TPU v7x, 8 devices: a whole 2x2x1 slice. The times are simulated.
8 devices in a mesh: dp: 2 (over y, z), tp: 4 (over x, core).
Axes of the slice: x: 2, y: 2, z: 1, core: 2. Of those that a mesh axis runs over, the one named last changes fastest.
Arguments:
- x: bfloat16 [1280, 6656], P(('dp', 'tp')), parts along dimension 0
- w_gate: bfloat16 [6656, 17920], P(None, 'tp')
- w_up: bfloat16 [6656, 17920], P(None, 'tp')
- w_down: bfloat16 [17920, 6656], P('tp')
Outputs:
- output: bfloat16 [1280, 6656], P(('dp', 'tp')), parts along dimension 0
There are 2 independent parts. A program takes and returns all parts, laid end to end along the dimension named above; an argument that names none is the same for every part.
All inputs are finite; a program needn't handle non-finite values.
Results may differ from a plain program's by a relative error of at most 0.016.
Values are sent between devices in bfloat16 or wider.
A program may use at most 2 GiB of HBM per device.

v0:
```python
import jax
import jax.numpy as jnp
from jax import lax
from jax.sharding import PartitionSpec as P


def solution(mesh):
    def step(x, w_gate, w_up, w_down):
        rows = lax.all_gather(x, "tp", axis=0, tiled=True)
        gate = jnp.dot(rows, w_gate, preferred_element_type=jnp.float32)
        up = jnp.dot(rows, w_up, preferred_element_type=jnp.float32)
        hidden = (jax.nn.silu(gate) * up).astype(jnp.bfloat16)
        term = jnp.dot(hidden, w_down, preferred_element_type=jnp.float32).astype(jnp.bfloat16)
        return lax.psum_scatter(term, "tp", scatter_dimension=0, tiled=True)

    return jax.shard_map(
        step,
        mesh=mesh,
        in_specs=(P(("dp", "tp"), None), P(None, "tp"), P(None, "tp"), P("tp", None)),
        out_specs=P(("dp", "tp"), None),
        check_vma=False,
    )
```

profile of v0, /device:TPU:0, one launch (start us, length us, event | category | flops | bytes accessed | tf_op | source)
XLA Modules:
  0.0 284.9 jit_solution(7208029009965639424)
XLA Ops:
  6.5 0.0 all-gather.2.cloned.1.call-start
  6.5 0.7 all-gather.2.cloned.1.call-update
  7.3 0.0 reduce-scatter.2.cloned.1.call-start
  7.3 60.9 %all-gather.2.cloned.1.call-done = bf16[640,6656]{1,0:T(8,128)(2,1)} async-done(((bf16[160,6656]{1,0:T(8,128)(2,1)}), bf16[640,6656]{1,0:T(8,128)(2,1)}) %all-gather.2.cloned.1.call-update) | async-done | bytes 8519696 | tf_op jit(solution)/shard_map/all_gather | solution.py:9
  68.2 0.0 copy-start
  68.2 51.2 %fusion = f32[640,4480]{1,0:T(8,128)} fusion(bf16[640,6656]{1,0:T(8,128)(2,1)} %all-gather.2.cloned.1.call-done, bf16[6656,4480]{1,0:T(8,128)(2,1)} %param.5), kind=kOutput, calls=%fused_computation.2 | convolution fusion | flops 38168166400 | bytes 79626240 | tf_op jit(solution)/shard_map/dot_general | solution.py:10
  119.4 0.0 copy-done
  119.4 45.9 %multiply_convert_fusion = bf16[640,4480]{1,0:T(8,128)(2,1)S(1)} fusion(f32[640,4480]{1,0:T(8,128)} %fusion, bf16[640,6656]{1,0:T(8,128)(2,1)S(1)} %copy-done, bf16[6656,4480]{1,0:T(8,128)(2,1)} %param.6), kind=kOutput, calls=%fused_computation | convolution fusion | flops 38185369600 | bytes 85360640 | tf_op jit(solution)/shard_map/dot_general | solution.py:11
  165.2 46.7 %convolution_convert_fusion = bf16[640,6656]{1,0:T(8,128)(2,1)} fusion(bf16[640,4480]{1,0:T(8,128)(2,1)S(1)} %multiply_convert_fusion, bf16[4480,6656]{1,0:T(8,128)(2,1)} %param.7), kind=kOutput, calls=%fused_computation.1 | convolution fusion | flops 38172426240 | bytes 73891840 | tf_op jit(solution)/shard_map/dot_general | solution.py:13
  212.0 0.0 reduce-scatter.2.cloned.1.call-update
  212.0 66.1 %reduce-scatter.2.cloned.1.call-done = bf16[160,6656]{1,0:T(8,128)(2,1)} async-done(((bf16[640,6656]{1,0:T(8,128)(2,1)}), bf16[160,6656]{1,0:T(8,128)(2,1)}) %reduce-scatter.2.cloned.1.call-update) | async-done | bytes 2129936 | tf_op jit(solution)/shard_map/reduce_scatter | solution.py:14
Async XLA Ops:
  6.5 61.7 %all-gather.2.cloned.1.call-start = ((), (), s32[]{:S(2)}) async-start(), calls=%async_computation.1 | async-start | bytes 10649600 | tf_op jit(solution)/shard_map/all_gather | solution.py:9
  7.3 270.9 %reduce-scatter.2.cloned.1.call-start = ((), (), s32[]{:S(2)}) async-start(), calls=%async_computation.2 | async-start | bytes 10649600 | tf_op jit(solution)/shard_map/reduce_scatter | solution.py:14
  68.2 51.2 %copy-start = (bf16[640,6656]{1,0:T(8,128)(2,1)S(1)}, bf16[640,6656]{1,0:T(8,128)(2,1)}, u32[]{:S(2)}) copy-start(bf16[640,6656]{1,0:T(8,128)(2,1)} %all-gather.2.cloned.1.call-done) | copy-start | bytes 25559044
Sparse Core Ops, SparseCore 0:
  8.9 59.2 all-gather.1
  212.1 65.9 reduce-scatter.1
where the time goes:
time: 285 us
  matrix products  144 us (51%)
  waiting for transfers between devices  128 us (45%)
  between operations  13.4 us (5%)
    reduce_scatter x1, waiting for transfers between devices, step(): return lax.psum_scatter(term, 'tp', scatter_dimension=0, tiled=True)  66.1 us
    all_gather x1, waiting for transfers between devices, step(): rows = lax.all_gather(x, 'tp', axis=0, tiled=True)  60.9 us
    dot_general x1, matrix products, step(): gate = jnp.dot(rows, w_gate, preferred_element_type=jnp.float32)  51.2 us
    dot_general x1, matrix products, step(): jnp.dot(hidden, w_down, preferred_element_type=jnp.float32)  46.7 us
    dot_general x1, matrix products, step(): up = jnp.dot(rows, w_up, preferred_element_type=jnp.float32)  45.9 us
  transfers between devices with their start and end apart: 2, of which 2 were waited for; matrix products, arithmetic and copies ran while one was open for 0% of the time, Pallas kernels for 0%

commit v1 on v0

v1 whole, which is shorter than its diff:
```python
import functools

import jax
import jax.numpy as jnp
from jax import lax
from jax.experimental import pallas as pl
from jax.experimental.pallas import tpu as pltpu
from jax.sharding import PartitionSpec as P

MESH = pl.DeviceIdType.MESH
F32 = jnp.float32
BF16 = jnp.bfloat16

D = 6656
FF = 4480
ROWS = 160
NT = 256
NFULL = FF // NT
TAIL = FF - NFULL * NT
CW = 512
NC = D // CW
SLOTS = 3


def kernel(
    x_ref, wg_ref, wu_ref, wd_ref, y_ref,
    xall, hid, wbuf, wdbuf,
    kept, send_r, recv_r, stage, recv_x, send_l, recv_l, acc_l,
    xsem, wsem, wdsem, tailsem,
    ag_send, ag_recv, fw_send, fw_recv, px_send, px_recv,
    rr_send, rr_recv, rx_send, rx_recv, rl_send, rl_recv, ysem,
):
    dp = lax.axis_index("dp")
    tp = lax.axis_index("tp")
    core = lax.rem(tp, 2)
    chip = lax.div(tp, 2)
    partner = (dp, chip * 2 + (1 - core))
    remote = (dp, (1 - chip) * 2 + core)

    def gate_up_copies(step, slot):
        col = pl.ds(pl.multiple_of(lax.rem(step, NFULL) * NT, NT), NT)
        return [
            pltpu.make_async_copy(w.at[:, col], wbuf.at[slot, j], wsem.at[slot, j])
            for j, w in enumerate((wg_ref, wu_ref))
        ]

    def down_copy(n, slot):
        col = pl.ds(pl.multiple_of(n * CW, CW), CW)
        return pltpu.make_async_copy(wd_ref.at[:, col], wdbuf.at[slot], wdsem.at[slot])

    def tail_copies():
        slot = (2 * NFULL) % SLOTS
        return [
            pltpu.make_async_copy(
                w.at[:, pl.ds(NFULL * NT, TAIL)],
                wbuf.at[slot, 0, :, pl.ds(j * TAIL, TAIL)],
                tailsem.at[j],
            )
            for j, w in enumerate((wg_ref, wu_ref))
        ]

    own = pltpu.make_async_copy(x_ref, xall.at[pl.ds(0, ROWS)], xsem)
    own.start()
    for s in range(SLOTS - 1):
        for c in gate_up_copies(s, s):
            c.start()

    barrier = pltpu.get_barrier_semaphore()
    for other in (partner, remote):
        pl.semaphore_signal(barrier, inc=1, device_id=other, device_id_type=MESH)
    pl.semaphore_wait(barrier, 2)

    to_partner = pltpu.make_async_remote_copy(
        src_ref=x_ref, dst_ref=xall.at[pl.ds(ROWS, ROWS)],
        send_sem=px_send, recv_sem=px_recv,
        device_id=partner, device_id_type=MESH,
    )
    to_partner.start()

    def chunk(c):
        return pl.ds(pl.multiple_of(c * CW, CW), CW)

    def gather_copy(c):
        return pltpu.make_async_remote_copy(
            src_ref=x_ref.at[:, chunk(c)],
            dst_ref=xall.at[pl.ds(2 * ROWS, ROWS), chunk(c)],
            send_sem=ag_send.at[c], recv_sem=ag_recv.at[c],
            device_id=remote, device_id_type=MESH,
        )

    def forward_copy(c):
        return pltpu.make_async_remote_copy(
            src_ref=xall.at[pl.ds(2 * ROWS, ROWS), chunk(c)],
            dst_ref=xall.at[pl.ds(3 * ROWS, ROWS), chunk(c)],
            send_sem=fw_send.at[c], recv_sem=fw_recv.at[c],
            device_id=partner, device_id_type=MESH,
        )

    @pl.loop(0, NC)
    def _(c):
        gather_copy(c).start()

    own.wait()
    to_partner.wait_recv()

    def forward(c):
        gather_copy(c).wait_recv()
        forward_copy(c).start()

    def gate_up(rows, step):
        slot = lax.rem(step, SLOTS)
        for c in gate_up_copies(step, slot):
            c.wait()
        ahead = step + SLOTS - 1

        @pl.when(ahead < 2 * NFULL)
        def _():
            for c in gate_up_copies(ahead, lax.rem(ahead, SLOTS)):
                c.start()

        g = jnp.dot(xall[rows], wbuf[slot, 0], preferred_element_type=F32)
        u = jnp.dot(xall[rows], wbuf[slot, 1], preferred_element_type=F32)
        col = pl.ds(pl.multiple_of(lax.rem(step, NFULL) * NT, NT), NT)
        hid[rows, col] = (jax.nn.silu(g) * u).astype(BF16)

    @pl.loop(0, NFULL)
    def _(i):
        gate_up(pl.ds(0, 2 * ROWS), i)
        lo = lax.div(2 * i, 3)
        hi = lax.div(2 * i + 2, 3)

        @pl.when(hi > lo)
        def _():
            forward(lo)

    for c in range((2 * NFULL) // 3, NC):
        forward(c)
    for c in range(NC):
        forward_copy(c).wait_recv()

    @pl.loop(0, NFULL)
    def _(i):
        gate_up(pl.ds(2 * ROWS, 2 * ROWS), NFULL + i)

        @pl.when(i == NFULL - 2)
        def _():
            for c in tail_copies():
                c.start()

        @pl.when(i == NFULL - 1)
        def _():
            for n in range(2):
                down_copy(n, n).start()

    for c in tail_copies():
        c.wait()
    for r in (pl.ds(2 * ROWS, 2 * ROWS), pl.ds(0, 2 * ROWS)):
        gu = jnp.dot(xall[r], wbuf[(2 * NFULL) % SLOTS, 0], preferred_element_type=F32)
        hid[r, pl.ds(NFULL * NT, TAIL)] = (
            jax.nn.silu(gu[:, :TAIL]) * gu[:, TAIL:]
        ).astype(BF16)

    def side_copy(src, dst, n, ssem, rsem, dev):
        return pltpu.make_async_remote_copy(
            src_ref=src, dst_ref=dst.at[n], send_sem=ssem.at[n], recv_sem=rsem.at[n],
            device_id=dev, device_id_type=MESH,
        )

    def r_copy(n):
        return side_copy(send_r.at[lax.rem(n, 2)], recv_r, n, rr_send, rr_recv, partner)

    def l_copy(n):
        return side_copy(send_l.at[lax.rem(n, 2)], recv_l, n, rl_send, rl_recv, partner)

    def x_copy(n):
        return side_copy(stage.at[n], recv_x, n, rx_send, rx_recv, remote)

    @pl.loop(0, NC)
    def _(n):
        slot = lax.rem(n, 2)
        down_copy(n, slot).wait()

        @pl.when(n >= 2)
        def _():
            r_copy(n - 2).wait_send()
            l_copy(n - 2).wait_send()

        pr = jnp.dot(hid[pl.ds(2 * ROWS, 2 * ROWS)], wdbuf[slot], preferred_element_type=F32)
        kept[...] = pr[:ROWS]
        send_r[slot] = pr[ROWS:].astype(BF16)
        r_copy(n).start()
        pll = jnp.dot(hid[pl.ds(0, 2 * ROWS)], wdbuf[slot], preferred_element_type=F32)
        acc_l[n] = pll[:ROWS]
        send_l[slot] = pll[ROWS:].astype(BF16)
        l_copy(n).start()

        @pl.when(n + 2 < NC)
        def _():
            down_copy(n + 2, slot).start()

        r_copy(n).wait_recv()
        stage[n] = (kept[...] + recv_r[n].astype(F32)).astype(BF16)
        x_copy(n).start()

    def y_copy(n):
        return pltpu.make_async_copy(stage.at[n], y_ref.at[:, chunk(n)], ysem.at[n])

    @pl.loop(0, NC)
    def _(n):
        l_copy(n).wait_recv()
        x_copy(n).wait()
        total = acc_l[n] + recv_l[n].astype(F32) + recv_x[n].astype(F32)
        stage[n] = total.astype(BF16)
        y_copy(n).start()

    for n in (NC - 2, NC - 1):
        r_copy(n).wait_send()
        l_copy(n).wait_send()
    to_partner.wait_send()

    @pl.loop(0, NC)
    def _(c):
        gather_copy(c).wait_send()
        forward_copy(c).wait_send()
        y_copy(c).wait()


def solution(mesh):
    dma = pltpu.SemaphoreType.DMA

    def step(x, w_gate, w_up, w_down):
        return pl.pallas_call(
            kernel,
            out_shape=jax.ShapeDtypeStruct((ROWS, D), BF16),
            in_specs=[pl.BlockSpec(memory_space=pl.ANY)] * 4,
            out_specs=pl.BlockSpec(memory_space=pl.ANY),
            scratch_shapes=[
                pltpu.VMEM((4 * ROWS, D), BF16),
                pltpu.VMEM((4 * ROWS, FF), BF16),
                pltpu.VMEM((SLOTS, 2, D, NT), BF16),
                pltpu.VMEM((2, FF, CW), BF16),
                pltpu.VMEM((ROWS, CW), F32),
                pltpu.VMEM((2, ROWS, CW), BF16),
                pltpu.VMEM((NC, ROWS, CW), BF16),
                pltpu.VMEM((NC, ROWS, CW), BF16),
                pltpu.VMEM((NC, ROWS, CW), BF16),
                pltpu.VMEM((2, ROWS, CW), BF16),
                pltpu.VMEM((NC, ROWS, CW), BF16),
                pltpu.VMEM((NC, ROWS, CW), F32),
                dma, dma((SLOTS, 2)), dma((2,)), dma((2,)),
                dma((NC,)), dma((NC,)), dma((NC,)), dma((NC,)), dma, dma,
                dma((NC,)), dma((NC,)), dma((NC,)), dma((NC,)), dma((NC,)), dma((NC,)),
                dma((NC,)),
            ],
            compiler_params=pltpu.CompilerParams(
                collective_id=0, has_side_effects=True, vmem_limit_bytes=67043328
            ),
            cost_estimate=pl.CostEstimate(
                flops=6 * 4 * ROWS * D * FF, bytes_accessed=3 * D * FF * 2, transcendentals=4 * ROWS * FF
            ),
        )(x, w_gate, w_up, w_down)

    return jax.shard_map(
        step,
        mesh=mesh,
        in_specs=(P(("dp", "tp"), None), P(None, "tp"), P(None, "tp"), P("tp", None)),
        out_specs=P(("dp", "tp"), None),
        check_vma=False,
    )
```

time: 285 us -> 151 us (0.53)
  Pallas kernels: 0 us -> 148 us
  matrix products: 144 us -> 0 us
  waiting for transfers between devices: 128 us -> 0 us
  between operations: 13.4 us -> 0.01 us
  local copies, waits for them, and re-layouts: 0.01 us -> 3.07 us
    pallas_call x0 -> x1, Pallas kernels: none -> 148 us  [step(): pl.pallas_call(kernel, out_shape=jax.ShapeDtypeStruct((ROWS, D), BF16), i...]
    dot_general x3 -> x0, matrix products: 144 us -> none  [the longest x1 51.2 us: step(): gate = jnp.dot(rows, w_gate, preferred_element_type=jnp.float32)]
    reduce_scatter x1 -> x0, waiting for transfers between devices: 66.1 us -> none  [step(): return lax.psum_scatter(term, 'tp', scatter_dimension=0, tiled=True)]
    all_gather x1 -> x0, waiting for transfers between devices: 60.9 us -> none  [step(): rows = lax.all_gather(x, 'tp', axis=0, tiled=True)]
    unnamed x2 -> x1, local copies, waits for them, and re-layouts: 0.01 us -> 3.07 us
  transfers between devices with their start and end apart: 2 -> 0, of which waited for: 2 -> 0; matrix products, arithmetic and copies ran while one was open for 0% -> 0% of each run, Pallas kernels for 0% -> 0%
where the time goes in v1:
time: 151 us
  Pallas kernels  148 us (98%)
  local copies, waits for them, and re-layouts  3.07 us (2%)
    pallas_call x1, Pallas kernels, step(): pl.pallas_call(kernel, out_shape=jax.ShapeDtypeStruct((ROWS, D), BF16), i...  148 us
    unnamed x1, local copies, waits for them, and re-layouts  3.07 us

profile of v1, /device:TPU:0, one launch (start us, length us, event | category | flops | bytes accessed | tf_op | source)
XLA Modules:
  0.0 150.7 jit_solution(4615597665529255287)
XLA Ops:
  0.0 147.6 %shard_map.46 = bf16[160,6656]{1,0:T(8,128)(2,1)} custom-call(bf16[160,6656]{1,0:T(8,128)(2,1)} %x_ref.1, bf16[6656,4480]{1,0:T(8,128)(2,1)} %wg_ref.1, bf16[6656,4480]{1,0:T(8,128)(2,1)} %wu_ref.1, bf16[4480,6656]{1,0:T(8,128)(2,1)} %wd_ref.1), custom_call_target="tpu_custom_call" | custom-call | flops 114504499200 | bytes 178913280 | tf_op jit(solution)/shard_map/pallas_call | solution.py:232
  147.6 3.1 %copy.6 = bf16[160,6656]{1,0:T(8,128)(2,1)} copy(bf16[160,6656]{1,0:T(8,128)(2,1)} %shard_map.46) | data formatting | bytes 4259840

commit v2 on v1

v2 whole, which is shorter than its diff:
```python
import functools

import jax
import jax.numpy as jnp
from jax import lax
from jax.experimental import pallas as pl
from jax.experimental.pallas import tpu as pltpu
from jax.sharding import PartitionSpec as P

MESH = pl.DeviceIdType.MESH
F32 = jnp.float32
BF16 = jnp.bfloat16

D = 6656
FF = 4480
ROWS = 160
NT = 256
NFULL = FF // NT
TAIL = FF - NFULL * NT
CW = 512
NC = D // CW
SLOTS = 3
HALF = D // 2
PAIRS = NFULL // 2
EARLY = 12
LATE = NFULL - EARLY


def kernel(
    x_ref, wg_ref, wu_ref, wd_ref, y_ref,
    xall, hid, wbuf, acc,
    kept, send_r, recv_r, stage, recv_x, send_l, recv_l, acc_l,
    xsem, wsem,
    ag_send, ag_recv, fw_send, fw_recv, px_send, px_recv,
    rr_send, rr_recv, rx_send, rx_recv, rl_send, rl_recv, ysem,
):
    dp = lax.axis_index("dp")
    tp = lax.axis_index("tp")
    core = lax.rem(tp, 2)
    chip = lax.div(tp, 2)
    partner = (dp, chip * 2 + (1 - core))
    remote = (dp, (1 - chip) * 2 + core)

    def copies(parts, slot):
        return [
            pltpu.make_async_copy(src, wbuf.at[slot, j, pl.ds(row, src.shape[0]), pl.ds(c, src.shape[1])], wsem.at[slot, k])
            for k, (src, j, row, c) in enumerate(parts)
        ]

    def cols(ref, t):
        return ref.at[:, pl.ds(pl.multiple_of(t * NT, NT), NT)]

    def full(t, slot):
        return copies([(cols(w, t), j, 0, 0) for j, w in enumerate((wg_ref, wu_ref))], slot)

    def half(t, h, slot, tiles=2):
        return copies(
            [
                (cols(w.at[pl.ds(h * HALF, HALF)], t + q), j, q * HALF, 0)
                for q in range(tiles)
                for j, w in enumerate((wg_ref, wu_ref))
            ],
            slot,
        )

    def tail(slot):
        col = pl.ds(NFULL * NT, TAIL)
        return copies([(w.at[:, col], 0, 0, j * TAIL) for j, w in enumerate((wg_ref, wu_ref))], slot)

    def down(n, slot):
        return copies([(cols(wd_ref, 2 * n + j), j, 0, 0) for j in range(2)], slot)

    def start(cs):
        for c in cs:
            c.start()

    def wait(cs):
        for c in cs:
            c.wait()

    def slot_of(step):
        return lax.rem(step, SLOTS)

    own = pltpu.make_async_copy(x_ref, xall.at[pl.ds(0, ROWS)], xsem)
    own.start()
    for s in range(SLOTS - 1):
        start(full(s, s))

    barrier = pltpu.get_barrier_semaphore()
    for other in (partner, remote):
        pl.semaphore_signal(barrier, inc=1, device_id=other, device_id_type=MESH)
    pl.semaphore_wait(barrier, 2)

    to_partner = pltpu.make_async_remote_copy(
        src_ref=x_ref, dst_ref=xall.at[pl.ds(ROWS, ROWS)],
        send_sem=px_send, recv_sem=px_recv,
        device_id=partner, device_id_type=MESH,
    )
    to_partner.start()

    def chunk(c):
        return pl.ds(pl.multiple_of(c * CW, CW), CW)

    def gather_copy(c):
        return pltpu.make_async_remote_copy(
            src_ref=x_ref.at[:, chunk(c)],
            dst_ref=xall.at[pl.ds(2 * ROWS, ROWS), chunk(c)],
            send_sem=ag_send.at[c], recv_sem=ag_recv.at[c],
            device_id=remote, device_id_type=MESH,
        )

    def forward_copy(c):
        return pltpu.make_async_remote_copy(
            src_ref=xall.at[pl.ds(2 * ROWS, ROWS), chunk(c)],
            dst_ref=xall.at[pl.ds(3 * ROWS, ROWS), chunk(c)],
            send_sem=fw_send.at[c], recv_sem=fw_recv.at[c],
            device_id=partner, device_id_type=MESH,
        )

    @pl.loop(0, NC)
    def _(c):
        gather_copy(c).start()

    own.wait()
    to_partner.wait_recv()

    def forward(c):
        gather_copy(c).wait_recv()
        forward_copy(c).start()

    own_rows, far_rows = pl.ds(0, 2 * ROWS), pl.ds(2 * ROWS, 2 * ROWS)

    def dot(rows, ks, slot, j, at):
        return jnp.dot(
            xall[rows, ks], wbuf[slot, j, pl.ds(at, ks.size)], preferred_element_type=F32
        )

    def put(rows, t, g, u):
        hid[rows, pl.ds(pl.multiple_of(t * NT, NT), NT)] = (jax.nn.silu(g) * u).astype(BF16)

    def gate_up_own(t, slot):
        g, u = (dot(own_rows, pl.ds(0, D), slot, j, 0) for j in range(2))
        put(own_rows, t, g, u)

    def first_half(t, slot, tiles=2):
        for q in range(tiles):
            for j in range(2):
                acc[t + q, j] = dot(far_rows, pl.ds(0, HALF), slot, j, q * HALF)

    def second_half(t, slot, tiles=2):
        for q in range(tiles):
            g, u = (acc[t + q, j] + dot(far_rows, pl.ds(HALF, HALF), slot, j, q * HALF) for j in range(2))
            put(far_rows, t + q, g, u)

    def forward_at(i):
        lo = lax.div(2 * i, 3)

        @pl.when(lax.div(2 * i + 2, 3) > lo)
        def _():
            forward(lo)

    @pl.loop(0, EARLY)
    def _(i):
        slot, later = slot_of(i), slot_of(i + 2)
        wait(full(i, slot))

        @pl.when(i + 2 < EARLY)
        def _():
            start(full(i + 2, later))

        @pl.when(i + 2 >= EARLY)
        def _():
            start(half(2 * (i + 2 - EARLY), 0, later))

        gate_up_own(i, slot)
        forward_at(i)

    for c in range(7):
        forward_copy(c).wait_recv()

    S1 = EARLY

    @pl.loop(0, PAIRS)
    def _(p):
        slot, later = slot_of(S1 + p), slot_of(S1 + p + 2)
        wait(half(2 * p, 0, slot))

        @pl.when(p + 2 < PAIRS)
        def _():
            start(half(2 * p + 4, 0, later))

        @pl.when(p + 2 == PAIRS)
        def _():
            start(half(2 * PAIRS, 0, later, 1))

        @pl.when(p + 2 > PAIRS)
        def _():
            start(half(0, 1, later))

        first_half(2 * p, slot)
        forward_at(S1 + p)

    S2 = S1 + PAIRS
    wait(half(2 * PAIRS, 0, S2 % SLOTS, 1))
    start(half(2, 1, (S2 + 2) % SLOTS))
    first_half(2 * PAIRS, S2 % SLOTS, 1)
    for c in range(7, NC):
        forward_copy(c).wait_recv()

    S3 = S2 + 1

    @pl.loop(0, PAIRS)
    def _(p):
        slot, later = slot_of(S3 + p), slot_of(S3 + p + 2)
        wait(half(2 * p, 1, slot))

        @pl.when(p + 2 < PAIRS)
        def _():
            start(half(2 * p + 4, 1, later))

        @pl.when(p + 2 == PAIRS)
        def _():
            start(half(2 * PAIRS, 1, later, 1))

        @pl.when(p + 2 > PAIRS)
        def _():
            start(tail(later))

        second_half(2 * p, slot)

    S4 = S3 + PAIRS
    wait(half(2 * PAIRS, 1, S4 % SLOTS, 1))
    wait(tail((S4 + 1) % SLOTS))
    start(down(0, (S4 + 2) % SLOTS))
    second_half(2 * PAIRS, S4 % SLOTS, 1)
    for r in (far_rows, own_rows):
        gu = dot(r, pl.ds(0, D), (S4 + 1) % SLOTS, 0, 0)
        hid[r, pl.ds(NFULL * NT, TAIL)] = (
            jax.nn.silu(gu[:, :TAIL]) * gu[:, TAIL:]
        ).astype(BF16)
    S5 = S4 + 2
    start(full(EARLY, (S5 + 1) % SLOTS))

    def side_copy(src, dst, n, ssem, rsem, dev):
        return pltpu.make_async_remote_copy(
            src_ref=src, dst_ref=dst.at[n], send_sem=ssem.at[n], recv_sem=rsem.at[n],
            device_id=dev, device_id_type=MESH,
        )

    def r_copy(n):
        return side_copy(send_r.at[lax.rem(n, 2)], recv_r, n, rr_send, rr_recv, partner)

    def l_copy(n):
        m = lax.rem(n + NC - LATE, NC)
        return side_copy(send_l.at[lax.rem(m, 2)], recv_l, n, rl_send, rl_recv, partner)

    def x_copy(n):
        return side_copy(stage.at[n], recv_x, n, rx_send, rx_recv, remote)

    def term(rows, slot, j):
        return jnp.dot(hid[rows], wbuf[slot, j, pl.ds(0, FF)], preferred_element_type=F32)

    def down_far(n, slot):
        @pl.when(n >= 2)
        def _():
            r_copy(n - 2).wait_send()

        out = lax.rem(n, 2)
        for j in range(2):
            col = pl.ds(j * NT, NT)
            t = term(far_rows, slot, j)
            kept[:, col] = t[:ROWS]
            send_r[out, :, col] = t[ROWS:].astype(BF16)
        r_copy(n).start()

    def down_own(n, slot):
        m = lax.rem(n + NC - LATE, NC)

        @pl.when(m >= 2)
        def _():
            l_copy(lax.rem(n + NC - 2, NC)).wait_send()

        out = lax.rem(m, 2)
        for j in range(2):
            col = pl.ds(j * NT, NT)
            t = term(own_rows, slot, j)
            acc_l[n, :, col] = t[:ROWS]
            send_l[out, :, col] = t[ROWS:].astype(BF16)
        l_copy(n).start()

    def reduce_far(n):
        r_copy(n).wait_recv()
        stage[n] = (kept[...] + recv_r[n].astype(F32)).astype(BF16)
        x_copy(n).start()

    @pl.loop(0, LATE)
    def _(k):
        slot = slot_of(S5 + 2 * k)
        wait(down(k, slot))
        start(down(k + 1, slot_of(S5 + 2 * k + 2)))
        down_far(k, slot)
        slot = slot_of(S5 + 2 * k + 1)
        wait(full(EARLY + k, slot))

        @pl.when(k + 1 < LATE)
        def _():
            start(full(EARLY + k + 1, slot_of(S5 + 2 * k + 3)))

        @pl.when(k + 1 == LATE)
        def _():
            start(down(LATE + 1, slot_of(S5 + 2 * k + 3)))

        gate_up_own(EARLY + k, slot)
        reduce_far(k)

    S6 = S5 + 2 * LATE

    @pl.loop(LATE, NC)
    def _(n):
        slot = slot_of(S6 + n - LATE)
        wait(down(n, slot))
        start(down(lax.rem(n + 2, NC), slot_of(S6 + n - LATE + 2)))
        down_far(n, slot)
        down_own(n, slot)
        reduce_far(n)

    S7 = S6 + NC - LATE

    @pl.loop(0, LATE)
    def _(n):
        slot = slot_of(S7 + n)
        wait(down(n, slot))

        @pl.when(n + 2 < LATE)
        def _():
            start(down(n + 2, slot_of(S7 + n + 2)))

        down_own(n, slot)

    def y_copy(n):
        return pltpu.make_async_copy(stage.at[n], y_ref.at[:, chunk(n)], ysem.at[n])

    @pl.loop(0, NC)
    def _(n):
        l_copy(n).wait_recv()
        x_copy(n).wait()
        total = acc_l[n] + recv_l[n].astype(F32) + recv_x[n].astype(F32)
        stage[n] = total.astype(BF16)
        y_copy(n).start()

    for n in (NC - 2, NC - 1):
        r_copy(n).wait_send()
        l_copy((n + LATE) % NC).wait_send()
    to_partner.wait_send()

    @pl.loop(0, NC)
    def _(c):
        gather_copy(c).wait_send()
        forward_copy(c).wait_send()
        y_copy(c).wait()


def solution(mesh):
    dma = pltpu.SemaphoreType.DMA

    def step(x, w_gate, w_up, w_down):
        return pl.pallas_call(
            kernel,
            out_shape=jax.ShapeDtypeStruct((ROWS, D), BF16),
            in_specs=[pl.BlockSpec(memory_space=pl.ANY)] * 4,
            out_specs=pl.BlockSpec(memory_space=pl.ANY),
            scratch_shapes=[
                pltpu.VMEM((4 * ROWS, D), BF16),
                pltpu.VMEM((4 * ROWS, FF), BF16),
                pltpu.VMEM((SLOTS, 2, D, NT), BF16),
                pltpu.VMEM((NFULL, 2, 2 * ROWS, NT), F32),
                pltpu.VMEM((ROWS, CW), F32),
                pltpu.VMEM((2, ROWS, CW), BF16),
                pltpu.VMEM((NC, ROWS, CW), BF16),
                pltpu.VMEM((NC, ROWS, CW), BF16),
                pltpu.VMEM((NC, ROWS, CW), BF16),
                pltpu.VMEM((2, ROWS, CW), BF16),
                pltpu.VMEM((NC, ROWS, CW), BF16),
                pltpu.VMEM((NC, ROWS, CW), F32),
                dma, dma((SLOTS, 4)),
                dma((NC,)), dma((NC,)), dma((NC,)), dma((NC,)), dma, dma,
                dma((NC,)), dma((NC,)), dma((NC,)), dma((NC,)), dma((NC,)), dma((NC,)),
                dma((NC,)),
            ],
            compiler_params=pltpu.CompilerParams(
                collective_id=0, has_side_effects=True, vmem_limit_bytes=67043328
            ),
            cost_estimate=pl.CostEstimate(
                flops=6 * 4 * ROWS * D * FF, bytes_accessed=3 * D * FF * 2, transcendentals=4 * ROWS * FF
            ),
        )(x, w_gate, w_up, w_down)

    return jax.shard_map(
        step,
        mesh=mesh,
        in_specs=(P(("dp", "tp"), None), P(None, "tp"), P(None, "tp"), P("tp", None)),
        out_specs=P(("dp", "tp"), None),
        check_vma=False,
    )
```

time: 151 us -> 144 us (0.954)
  Pallas kernels: 148 us -> 141 us
    pallas_call x1, Pallas kernels: 148 us -> 141 us  [step(): pl.pallas_call(kernel, out_shape=jax.ShapeDtypeStruct((ROWS, D), BF16), i...]
where the time goes in v2:
time: 144 us
  Pallas kernels  141 us (98%)
  local copies, waits for them, and re-layouts  3.07 us (2%)
    pallas_call x1, Pallas kernels, step(): pl.pallas_call(kernel, out_shape=jax.ShapeDtypeStruct((ROWS, D), BF16), i...  141 us
    unnamed x1, local copies, waits for them, and re-layouts  3.07 us

profile of v2, /device:TPU:0, one launch (start us, length us, event | category | flops | bytes accessed | tf_op | source)
XLA Modules:
  0.0 143.8 jit_solution(17915539001738134392)
XLA Ops:
  0.0 140.7 %shard_map.46 = bf16[160,6656]{1,0:T(8,128)(2,1)} custom-call(bf16[160,6656]{1,0:T(8,128)(2,1)} %x_ref.1, bf16[6656,4480]{1,0:T(8,128)(2,1)} %wg_ref.1, bf16[6656,4480]{1,0:T(8,128)(2,1)} %wu_ref.1, bf16[4480,6656]{1,0:T(8,128)(2,1)} %wd_ref.1), custom_call_target="tpu_custom_call" | custom-call | flops 114504499200 | bytes 178913280 | tf_op jit(solution)/shard_map/pallas_call | solution.py:367
  140.7 3.1 %copy.6 = bf16[160,6656]{1,0:T(8,128)(2,1)} copy(bf16[160,6656]{1,0:T(8,128)(2,1)} %shard_map.46) | data formatting | bytes 4259840

commit v3 on v2

v3 whole, which is shorter than its diff:
```python
import functools

import jax
import jax.numpy as jnp
from jax import lax
from jax.experimental import pallas as pl
from jax.experimental.pallas import tpu as pltpu
from jax.sharding import PartitionSpec as P

MESH = pl.DeviceIdType.MESH
F32 = jnp.float32
BF16 = jnp.bfloat16

D = 6656
FF = 4480
ROWS = 160
NT = 256
NFULL = FF // NT
TAIL = FF - NFULL * NT
CW = 512
NC = D // CW
NX = D // NT
SLOTS = 4
HALF = D // 2
PAIRS = NFULL // 2
EARLY = 12
LATE = NFULL - EARLY - 1
S1 = EARLY
S2 = S1 + PAIRS
S3 = S2 + 2
S4 = S3 + PAIRS
S5 = S4 + 2


def kernel(
    x_ref, wg_ref, wu_ref, wd_ref, y_ref,
    xall, hid, wbuf, acc,
    kept, send_r, recv_r, stage, recv_x, send_l, recv_l,
    xsem, wsem,
    ag_send, ag_recv, fw_send, fw_recv, px_send, px_recv,
    rr_send, rr_recv, rx_send, rx_recv, rl_send, rl_recv, ysem,
):
    dp = lax.axis_index("dp")
    tp = lax.axis_index("tp")
    core = lax.rem(tp, 2)
    chip = lax.div(tp, 2)
    partner = (dp, chip * 2 + (1 - core))
    remote = (dp, (1 - chip) * 2 + core)

    def copies(parts, slot):
        return [
            pltpu.make_async_copy(src, wbuf.at[slot, j, pl.ds(row, src.shape[0]), pl.ds(c, src.shape[1])], wsem.at[slot, k])
            for k, (src, j, row, c) in enumerate(parts)
        ]

    def cols(ref, t):
        return ref.at[:, pl.ds(pl.multiple_of(t * NT, NT), NT)]

    def halves(pick, slot):
        parts = []
        for q in range(2):
            h, t = pick(q)
            row = pl.ds(pl.multiple_of(h * HALF, HALF), HALF)
            parts += [(cols(w.at[row], t), j, q * HALF, 0) for j, w in enumerate((wg_ref, wu_ref))]
        return copies(parts, slot)

    def full(t, slot):
        return halves(lambda q: (q, t), slot)

    def fetch(step):
        def pick(q):
            own = (step < S1) | (step == S3 - 1)
            p = step - jnp.where(step >= S3, S3, S1)
            h = jnp.where(own, q, jnp.where(step >= S3, 1, 0))
            t = jnp.where(own, jnp.minimum(step, EARLY), jnp.minimum(2 * p + q, NFULL - 1))
            return h, t

        return halves(pick, slot_of(step))

    def tail(slot):
        col = pl.ds(NFULL * NT, TAIL)
        return copies([(w.at[:, col], 0, 0, j * TAIL) for j, w in enumerate((wg_ref, wu_ref))], slot)

    def down(n, slot):
        return copies([(cols(wd_ref, 2 * n + j), j, 0, 0) for j in range(2)], slot)

    def start(cs):
        for c in cs:
            c.start()

    def wait(cs):
        for c in cs:
            c.wait()

    def slot_of(step):
        return lax.rem(step, SLOTS)

    own = pltpu.make_async_copy(x_ref, xall.at[pl.ds(0, ROWS)], xsem)
    own.start()
    for s in range(SLOTS - 1):
        start(full(s, s))

    barrier = pltpu.get_barrier_semaphore()
    for other in (partner, remote):
        pl.semaphore_signal(barrier, inc=1, device_id=other, device_id_type=MESH)
    pl.semaphore_wait(barrier, 2)

    to_partner = pltpu.make_async_remote_copy(
        src_ref=x_ref, dst_ref=xall.at[pl.ds(ROWS, ROWS)],
        send_sem=px_send, recv_sem=px_recv,
        device_id=partner, device_id_type=MESH,
    )
    to_partner.start()

    def chunk(c):
        return pl.ds(pl.multiple_of(c * CW, CW), CW)

    def piece(c):
        return pl.ds(pl.multiple_of(c * NT, NT), NT)

    def gather_copy(c):
        return pltpu.make_async_remote_copy(
            src_ref=x_ref.at[:, piece(c)],
            dst_ref=xall.at[pl.ds(2 * ROWS, ROWS), piece(c)],
            send_sem=ag_send.at[c], recv_sem=ag_recv.at[c],
            device_id=remote, device_id_type=MESH,
        )

    def forward_copy(c):
        return pltpu.make_async_remote_copy(
            src_ref=xall.at[pl.ds(2 * ROWS, ROWS), piece(c)],
            dst_ref=xall.at[pl.ds(3 * ROWS, ROWS), piece(c)],
            send_sem=fw_send.at[c], recv_sem=fw_recv.at[c],
            device_id=partner, device_id_type=MESH,
        )

    @pl.loop(0, NX)
    def _(c):
        gather_copy(c).start()

    own.wait()
    to_partner.wait_recv()

    def forward(c):
        gather_copy(c).wait_recv()
        forward_copy(c).start()

    own_rows, far_rows = pl.ds(0, 2 * ROWS), pl.ds(2 * ROWS, 2 * ROWS)

    def dot(rows, ks, slot, j, at):
        return jnp.dot(
            xall[rows, ks], wbuf[slot, j, pl.ds(at, ks.size)], preferred_element_type=F32
        )

    def put(rows, t, g, u):
        hid[rows, pl.ds(pl.multiple_of(t * NT, NT), NT)] = (jax.nn.silu(g) * u).astype(BF16)

    def gate_up_own(t, slot):
        g, u = (dot(own_rows, pl.ds(0, D), slot, j, 0) for j in range(2))
        put(own_rows, t, g, u)

    def first_half(t, slot, tiles=2):
        for q in range(tiles):
            for j in range(2):
                acc[t + q, j] = dot(far_rows, pl.ds(0, HALF), slot, j, q * HALF)

    def second_half(t, slot, tiles=2):
        for q in range(tiles):
            g, u = (acc[t + q, j] + dot(far_rows, pl.ds(HALF, HALF), slot, j, q * HALF) for j in range(2))
            put(far_rows, t + q, g, u)

    def forward_at(k):
        @pl.loop(lax.div(5 * k + 1, 2) * jnp.minimum(k, 1), lax.div(5 * k + 6, 2))
        def _(c):
            forward(c)

    def arrived(lo, hi):
        @pl.loop(lo, hi)
        def _(c):
            forward_copy(c).wait_recv()

    def two_steps(i, work, ahead=None):
        s0, s1 = slot_of(i), slot_of(i + 1)
        wait(fetch(i))
        wait(fetch(i + 1))
        start(ahead[0] if ahead else fetch(i + 3))
        work(i, s0)
        start(ahead[1] if ahead else fetch(i + 4))
        work(i + 1, s1)

    @pl.loop(0, EARLY // 2)
    def _(k):
        two_steps(2 * k, gate_up_own)
        forward_at(k)

    arrived(0, NX // 2)

    @pl.loop(0, PAIRS // 2)
    def _(k):
        two_steps(S1 + 2 * k, lambda i, slot: first_half(2 * (i - S1), slot))
        forward_at(EARLY // 2 + k)

    wait(fetch(S2))
    start(fetch(S2 + 3))
    first_half(2 * PAIRS, S2 % SLOTS, 1)
    forward(NX - 1)

    wait(fetch(S2 + 1))
    start(fetch(S2 + 4))
    gate_up_own(EARLY, (S2 + 1) % SLOTS)
    arrived(NX // 2, NX)

    def second(i, slot):
        second_half(2 * (i - S3), slot)

    @pl.loop(0, PAIRS // 2 - 1)
    def _(k):
        two_steps(S3 + 2 * k, second)

    two_steps(S4 - 2, second, (tail((S4 + 1) % SLOTS), down(0, S5 % SLOTS)))
    wait(fetch(S4))
    start(down(1, (S5 + 1) % SLOTS))
    second_half(2 * PAIRS, S4 % SLOTS, 1)
    wait(tail((S4 + 1) % SLOTS))
    start(down(2, (S5 + 2) % SLOTS))
    for r in (far_rows, own_rows):
        gu = dot(r, pl.ds(0, D), (S4 + 1) % SLOTS, 0, 0)
        hid[r, pl.ds(NFULL * NT, TAIL)] = (
            jax.nn.silu(gu[:, :TAIL]) * gu[:, TAIL:]
        ).astype(BF16)

    def side_copy(src, dst, n, ssem, rsem, dev):
        return pltpu.make_async_remote_copy(
            src_ref=src, dst_ref=dst.at[n], send_sem=ssem.at[n], recv_sem=rsem.at[n],
            device_id=dev, device_id_type=MESH,
        )

    FAR = LATE + 2

    def turn(n):
        return lax.rem(n + NC - FAR, NC)

    def r_copy(n):
        return side_copy(send_r.at[lax.rem(n, 2)], recv_r, n, rr_send, rr_recv, partner)

    def l_copy(n):
        return side_copy(send_l.at[lax.rem(turn(n), 2)], recv_l, n, rl_send, rl_recv, partner)

    def x_copy(n):
        return side_copy(stage.at[n], recv_x, n, rx_send, rx_recv, remote)

    def y_copy(n):
        return pltpu.make_async_copy(stage.at[n], y_ref.at[:, chunk(n)], ysem.at[n])

    def term(rows, slot, j):
        return jnp.dot(hid[rows], wbuf[slot, j, pl.ds(0, FF)], preferred_element_type=F32)

    def ready_own(n):
        @pl.when(turn(n) >= 2)
        def _():
            l_copy(lax.rem(n + NC - 2, NC)).wait_send()

    def term_far(n, slot):
        for j in range(2):
            col = pl.ds(j * NT, NT)
            t = term(far_rows, slot, j)
            kept[lax.rem(n, 2), :, col] = t[:ROWS]
            send_r[lax.rem(n, 2), :, col] = t[ROWS:].astype(BF16)

    def term_own(n, slot):
        for j in range(2):
            t = term(own_rows, slot, j)
            acc[n, j, pl.ds(0, ROWS)] = t[:ROWS]
            send_l[lax.rem(turn(n), 2), :, pl.ds(j * NT, NT)] = t[ROWS:].astype(BF16)

    def reduce_far(n):
        r_copy(n).wait_recv()
        stage[n] = (kept[lax.rem(n, 2)] + recv_r[n].astype(F32)).astype(BF16)
        x_copy(n).start()

    def finish(n):
        l_copy(n).wait_recv()
        x_copy(n).wait()
        for j in range(2):
            col = pl.ds(j * NT, NT)
            stage[n, :, col] = (
                acc[n, j, pl.ds(0, ROWS)] + recv_l[n, :, col].astype(F32) + recv_x[n, :, col].astype(F32)
            ).astype(BF16)
        y_copy(n).start()

    wait(down(0, S5 % SLOTS))
    start(full(EARLY + 1, (S5 + 3) % SLOTS))
    term_far(0, S5 % SLOTS)
    r_copy(0).start()
    wait(down(1, (S5 + 1) % SLOTS))
    start(down(3, (S5 + 4) % SLOTS))
    term_far(1, (S5 + 1) % SLOTS)
    r_copy(1).start()
    reduce_far(0)

    @pl.loop(0, LATE)
    def _(k):
        s = S5 + 2 + 2 * k
        slot = slot_of(s)
        wait(down(k + 2, slot))

        @pl.when(k + 1 < LATE)
        def _():
            start(full(EARLY + k + 2, slot_of(s + 3)))

        @pl.when(k + 1 == LATE)
        def _():
            start(down(FAR + 1, slot_of(s + 3)))

        r_copy(k).wait_send()
        term_far(k + 2, slot)
        r_copy(k + 2).start()
        reduce_far(k + 1)
        slot = slot_of(s + 1)
        wait(full(EARLY + k + 1, slot))
        start(down(jnp.where(k + 1 < LATE, k + 4, FAR + 2), slot_of(s + 4)))
        gate_up_own(EARLY + k + 1, slot)

    reduce_far(FAR - 1)
    S6 = S5 + FAR + LATE

    @pl.loop(FAR, NC)
    def _(n):
        s = S6 + n - FAR
        slot = slot_of(s)
        wait(down(n, slot))
        start(down(lax.rem(n + 3, NC), slot_of(s + 3)))
        r_copy(n - 2).wait_send()
        ready_own(n)
        term_far(n, slot)
        term_own(n, slot)
        r_copy(n).start()
        l_copy(n).start()

        @pl.when(n > FAR)
        def _():
            reduce_far(n - 1)

    S7 = S6 + NC - FAR

    @pl.loop(0, FAR)
    def _(n):
        slot = slot_of(S7 + n)
        wait(down(n, slot))

        @pl.when(n + 3 < FAR)
        def _():
            start(down(n + 3, slot_of(S7 + n + 3)))

        ready_own(n)
        term_own(n, slot)
        l_copy(n).start()

        @pl.when(n == 0)
        def _():
            reduce_far(NC - 1)

        @pl.when(n > 0)
        def _():
            finish(FAR + n - 1)

    for n in range(2 * FAR - 1, NC - 1):
        finish(n)

    @pl.loop(0, FAR - 1)
    def _(n):
        finish(n)

    finish(NC - 1)
    finish(FAR - 1)

    for n in (NC - 2, NC - 1):
        r_copy(n).wait_send()
        l_copy((n + FAR) % NC).wait_send()
    to_partner.wait_send()

    @pl.loop(0, NX)
    def _(c):
        gather_copy(c).wait_send()
        forward_copy(c).wait_send()

    @pl.loop(0, NC)
    def _(n):
        y_copy(n).wait()


PARTS = 10


def settle(y_ref, out_ref, buf, isem, osem):
    rows = [pl.ds(i * (ROWS // PARTS), ROWS // PARTS) for i in range(PARTS)]
    ins = [pltpu.make_async_copy(y_ref.at[r], buf.at[r], isem.at[i]) for i, r in enumerate(rows)]
    outs = [pltpu.make_async_copy(buf.at[r], out_ref.at[r], osem.at[i]) for i, r in enumerate(rows)]
    for c in ins:
        c.start()
    for c, o in zip(ins, outs):
        c.wait()
        o.start()
    for o in outs:
        o.wait()


def solution(mesh):
    dma = pltpu.SemaphoreType.DMA

    def step(x, w_gate, w_up, w_down):
        y = pl.pallas_call(
            kernel,
            out_shape=jax.ShapeDtypeStruct((ROWS, D), BF16),
            in_specs=[pl.BlockSpec(memory_space=pl.ANY)] * 4,
            out_specs=pl.BlockSpec(memory_space=pl.ANY),
            scratch_shapes=[
                pltpu.VMEM((4 * ROWS, D), BF16),
                pltpu.VMEM((4 * ROWS, FF), BF16),
                pltpu.VMEM((SLOTS, 2, D, NT), BF16),
                pltpu.VMEM((NFULL, 2, 2 * ROWS, NT), F32),
                pltpu.VMEM((2, ROWS, CW), F32),
                pltpu.VMEM((2, ROWS, CW), BF16),
                pltpu.VMEM((NC, ROWS, CW), BF16),
                pltpu.VMEM((NC, ROWS, CW), BF16),
                pltpu.VMEM((NC, ROWS, CW), BF16),
                pltpu.VMEM((2, ROWS, CW), BF16),
                pltpu.VMEM((NC, ROWS, CW), BF16),
                dma, dma((SLOTS, 4)),
                dma((NX,)), dma((NX,)), dma((NX,)), dma((NX,)), dma, dma,
                dma((NC,)), dma((NC,)), dma((NC,)), dma((NC,)), dma((NC,)), dma((NC,)),
                dma((NC,)),
            ],
            compiler_params=pltpu.CompilerParams(
                collective_id=0, has_side_effects=True, vmem_limit_bytes=67043328
            ),
            cost_estimate=pl.CostEstimate(
                flops=6 * 4 * ROWS * D * FF, bytes_accessed=3 * D * FF * 2, transcendentals=4 * ROWS * FF
            ),
        )(x, w_gate, w_up, w_down)
        return pl.pallas_call(
            settle,
            out_shape=jax.ShapeDtypeStruct((ROWS, D), BF16),
            in_specs=[pl.BlockSpec(memory_space=pl.ANY)],
            out_specs=pl.BlockSpec(memory_space=pl.ANY),
            scratch_shapes=[pltpu.VMEM((ROWS, D), BF16), dma((PARTS,)), dma((PARTS,))],
        )(y)

    return jax.shard_map(
        step,
        mesh=mesh,
        in_specs=(P(("dp", "tp"), None), P(None, "tp"), P(None, "tp"), P("tp", None)),
        out_specs=P(("dp", "tp"), None),
        check_vma=False,
    )
```

time: 144 us -> 140 us (0.972)
  local copies, waits for them, and re-layouts: 3.07 us -> 0 us
    pallas_call x1, Pallas kernels: 141 us -> 137 us  [step(): pl.pallas_call(kernel, out_shape=jax.ShapeDtypeStruct((ROWS, D), BF16), i...]
    unnamed x1 -> x0, local copies, waits for them, and re-layouts: 3.07 us -> none
    pallas_call x0 -> x1, Pallas kernels: none -> 2.53 us  [step(): pl.pallas_call(settle, out_shape=jax.ShapeDtypeStruct((ROWS, D), BF16), i...]
where the time goes in v3:
time: 140 us
  Pallas kernels  140 us (100%)
    pallas_call x1, Pallas kernels, step(): pl.pallas_call(kernel, out_shape=jax.ShapeDtypeStruct((ROWS, D), BF16), i...  137 us

profile of v3, /device:TPU:0, one launch (start us, length us, event | category | flops | bytes accessed | tf_op | source)
XLA Modules:
  0.0 139.8 jit_solution(17611354659064063294)
XLA Ops:
  0.0 137.2 %shard_map.46.y_ref = bf16[160,6656]{1,0:T(8,128)(2,1)} custom-call(bf16[160,6656]{1,0:T(8,128)(2,1)} %x_ref.1, bf16[6656,4480]{1,0:T(8,128)(2,1)} %wg_ref.1, bf16[6656,4480]{1,0:T(8,128)(2,1)} %wu_ref.1, bf16[4480,6656]{1,0:T(8,128)(2,1)} %wd_ref.1), custom_call_target="tpu_custom_call" | custom-call | flops 114504499200 | bytes 178913280 | tf_op jit(solution)/shard_map/pallas_call | solution.py:412
  137.2 2.5 %shard_map.47 = bf16[160,6656]{1,0:T(8,128)(2,1)} custom-call(bf16[160,6656]{1,0:T(8,128)(2,1)} %shard_map.46.y_ref), custom_call_target="tpu_custom_call" | custom-call | tf_op jit(solution)/shard_map/pallas_call | solution.py:441

commit v4 on v3

--- a/solution.py
+++ b/solution.py
@@ -138,9 +138,6 @@
     def _(c):
         gather_copy(c).start()
 
-    own.wait()
-    to_partner.wait_recv()
-
     def forward(c):
         gather_copy(c).wait_recv()
         forward_copy(c).start()
@@ -155,9 +152,9 @@
     def put(rows, t, g, u):
         hid[rows, pl.ds(pl.multiple_of(t * NT, NT), NT)] = (jax.nn.silu(g) * u).astype(BF16)
 
-    def gate_up_own(t, slot):
-        g, u = (dot(own_rows, pl.ds(0, D), slot, j, 0) for j in range(2))
-        put(own_rows, t, g, u)
+    def gate_up_own(t, slot, rows=own_rows):
+        g, u = (dot(rows, pl.ds(0, D), slot, j, 0) for j in range(2))
+        put(rows, t, g, u)
 
     def first_half(t, slot, tiles=2):
         for q in range(tiles):
@@ -188,7 +185,19 @@
         start(ahead[1] if ahead else fetch(i + 4))
         work(i + 1, s1)
 
-    @pl.loop(0, EARLY // 2)
+    own.wait()
+    wait(fetch(0))
+    gate_up_own(0, 0, pl.ds(0, ROWS))
+    to_partner.wait_recv()
+    wait(fetch(1))
+    start(fetch(3))
+    gate_up_own(0, 0, pl.ds(ROWS, ROWS))
+    start(fetch(4))
+    gate_up_own(1, 1)
+    for c in range(3):
+        forward(c)
+
+    @pl.loop(1, EARLY // 2)
     def _(k):
         two_steps(2 * k, gate_up_own)
         forward_at(k)
@@ -219,9 +228,9 @@
 
     two_steps(S4 - 2, second, (tail((S4 + 1) % SLOTS), down(0, S5 % SLOTS)))
     wait(fetch(S4))
+    wait(tail((S4 + 1) % SLOTS))
     start(down(1, (S5 + 1) % SLOTS))
     second_half(2 * PAIRS, S4 % SLOTS, 1)
-    wait(tail((S4 + 1) % SLOTS))
     start(down(2, (S5 + 2) % SLOTS))
     for r in (far_rows, own_rows):
         gu = dot(r, pl.ds(0, D), (S4 + 1) % SLOTS, 0, 0)

time: 140 us -> 140 us (level)
  no operation moved by 1% of the time
where the time goes in v4:
time: 140 us
  Pallas kernels  140 us (100%)
    pallas_call x1, Pallas kernels, step(): pl.pallas_call(kernel, out_shape=jax.ShapeDtypeStruct((ROWS, D), BF16), i...  137 us

profile of v4, /device:TPU:0, one launch (start us, length us, event | category | flops | bytes accessed | tf_op | source)
XLA Modules:
  0.0 140.1 jit_solution(16627330762910148319)
XLA Ops:
  0.0 137.3 %shard_map.46.y_ref = bf16[160,6656]{1,0:T(8,128)(2,1)} custom-call(bf16[160,6656]{1,0:T(8,128)(2,1)} %x_ref.1, bf16[6656,4480]{1,0:T(8,128)(2,1)} %wg_ref.1, bf16[6656,4480]{1,0:T(8,128)(2,1)} %wu_ref.1, bf16[4480,6656]{1,0:T(8,128)(2,1)} %wd_ref.1), custom_call_target="tpu_custom_call" | custom-call | flops 114504499200 | bytes 178913280 | tf_op jit(solution)/shard_map/pallas_call | solution.py:421
  137.4 2.5 %shard_map.47 = bf16[160,6656]{1,0:T(8,128)(2,1)} custom-call(bf16[160,6656]{1,0:T(8,128)(2,1)} %shard_map.46.y_ref), custom_call_target="tpu_custom_call" | custom-call | tf_op jit(solution)/shard_map/pallas_call | solution.py:450
